TPU v7x, 256 devices: a whole 4x4x8 slice. The times are simulated.
256 devices in a mesh: sx: 8 (over y, core), sy: 8 (over z), af: 4 (over x).
Axes of the slice: x: 4, y: 4, z: 8, core: 2. Of those that a mesh axis runs over, the one named last changes fastest.
Arguments:
- sky_maps: float32 [256, 256, 1024], P('sx', 'sy', 'af'), may hold values from -16 to 25
- validity: int32 [256, 256], P('sx', 'sy'), may hold values 0 or 1
- row_taps: float32 [1024, 65], P('af'), may hold values from -0.75 to 0.75
- column_taps: float32 [1024, 65], P('af'), may hold values from -0.75 to 0.75
- init_loadings: float32 [1024, 32], P('af'), may hold values from -0.1875 to 0.1875
Outputs:
- cleaned_maps: float32 [256, 256, 1024], P('sx', 'sy', 'af')
- loadings: float32 [1024, 32], P('af')
- noise_var: float32 [], replicated
All inputs are finite; a program needn't handle non-finite values. No bound on the sum of `validity` on one device may be relied on, other than what follows from the above.
Results may differ from a plain program's by a relative error of at most 0.0003.
Values sent between devices are 32-bit elements; how exact they have to be, the bound alone decides.
No kernel may reach another device: no remote copies, remote signals or barrier semaphores. Data moves between devices by JAX's collectives and lax.ppermute only.
A program may use at most 128 MiB of HBM per device.

v0:
```python
import math
import jax
import jax.numpy as jnp
from jax import lax
from jax.sharding import PartitionSpec as P

ITERS = 4
HIGHEST_PRECISION = lax.Precision.HIGHEST


def padded(block, sides, width):
    for axis, dim in sides:
        count = lax.axis_size(axis)
        forward = [(i, i + 1) for i in range(count - 1)]
        backward = [(target, source) for source, target in forward]
        low = lax.ppermute(
            lax.slice_in_dim(block, block.shape[dim] - width, None, axis=dim), axis, forward
        )
        high = lax.ppermute(lax.slice_in_dim(block, 0, width, axis=dim), axis, backward)
        block = jnp.concatenate([low, block, high], axis=dim)
    return block


def inverse_spd(matrix):
    identity = jnp.eye(matrix.shape[0], dtype=matrix.dtype)
    factor = jnp.linalg.cholesky(matrix)
    lower_inverse = lax.linalg.triangular_solve(factor, identity, left_side=True, lower=True)
    return jnp.dot(lower_inverse.T, lower_inverse, precision=HIGHEST_PRECISION)


def contract_rows(left_rows, right_rows):
    return lax.dot_general(
        left_rows, right_rows, (((0,), (0,)), ((), ())), precision=HIGHEST_PRECISION
    )


def correlate(extended, tap_table, out_length, along_dim):
    freq_count, tap_count = tap_table.shape
    block_size = math.gcd(freq_count, 32)
    in_length = extended.shape[along_dim]
    offsets = jnp.arange(in_length)[:, None] - jnp.arange(out_length)[None, :]
    one_hot = (offsets[None, :, :] == jnp.arange(tap_count)[:, None, None]).astype(jnp.float32)
    shape_out = list(extended.shape)
    shape_out[along_dim] = out_length
    filtered_all = jnp.zeros(tuple(shape_out), jnp.float32)

    def add_block(block_index, filtered_all):
        first_freq = block_index * block_size
        slab_part = lax.dynamic_slice_in_dim(extended, first_freq, block_size, 2)
        tap_block = lax.dynamic_slice_in_dim(tap_table, first_freq, block_size, 0)
        band_matrix = jnp.einsum("ft,tio->fio", tap_block, one_hot, precision=HIGHEST_PRECISION)
        if along_dim == 0:
            filtered = jnp.einsum(
                "icf,fio->ocf", slab_part, band_matrix, precision=HIGHEST_PRECISION
            )
        else:
            filtered = jnp.einsum(
                "rif,fio->rof", slab_part, band_matrix, precision=HIGHEST_PRECISION
            )
        return lax.dynamic_update_slice_in_dim(filtered_all, filtered, first_freq, 2)

    return lax.fori_loop(0, freq_count // block_size, add_block, filtered_all)


def body(sky_maps, validity, row_taps, column_taps, init_loadings):
    rows_here, cols_here, freqs_here = sky_maps.shape
    halo_width = (row_taps.shape[1] - 1) // 2
    masked = sky_maps * validity.astype(jnp.float32)[:, :, None]
    extended = padded(masked, (("sx", 0), ("sy", 1)), halo_width)
    smoothed = correlate(extended, row_taps, rows_here, 0)
    beamed = correlate(smoothed, column_taps, cols_here, 1)
    spectra = beamed.reshape(rows_here * cols_here, freqs_here)
    total_power = lax.psum(jnp.sum(spectra * spectra), ("sx", "sy", "af"))
    pixel_count = rows_here * cols_here * lax.axis_size("sx") * lax.axis_size("sy")
    freq_total = freqs_here * lax.axis_size("af")
    components = init_loadings.shape[1]
    identity = jnp.eye(components, dtype=jnp.float32)
    noise_var = jnp.float32(1.0)
    loadings = lax.all_gather(init_loadings, "af", axis=0, tiled=True)
    pixel_rows = lax.all_to_all(spectra, "af", split_axis=0, concat_axis=1, tiled=True)
    for iteration in range(ITERS):
        inverse = inverse_spd(contract_rows(loadings, loadings) + noise_var * identity)
        latent = jnp.dot(
            pixel_rows,
            jnp.dot(loadings, inverse, precision=HIGHEST_PRECISION),
            precision=HIGHEST_PRECISION,
        )
        cross_moment, second = lax.psum(
            (contract_rows(pixel_rows, latent), contract_rows(latent, latent)), ("sx", "sy", "af")
        )
        scaled = pixel_count * noise_var * inverse + second
        updated = jnp.dot(cross_moment, inverse_spd(scaled), precision=HIGHEST_PRECISION)
        new_gram = contract_rows(updated, updated)
        noise_var = (
            total_power - 2.0 * jnp.sum(updated * cross_moment) + jnp.sum(scaled * new_gram)
        ) / (pixel_count * freq_total)
        loadings = updated
    inverse = inverse_spd(contract_rows(loadings, loadings) + noise_var * identity)
    latent = jnp.dot(
        pixel_rows,
        jnp.dot(loadings, inverse, precision=HIGHEST_PRECISION),
        precision=HIGHEST_PRECISION,
    )
    cleaned_rows = pixel_rows - jnp.dot(latent, loadings.T, precision=HIGHEST_PRECISION)
    cleaned = lax.all_to_all(cleaned_rows, "af", split_axis=1, concat_axis=0, tiled=True)
    loadings_block = lax.dynamic_slice_in_dim(
        loadings, lax.axis_index("af") * freqs_here, freqs_here, 0
    )
    return (cleaned.reshape(rows_here, cols_here, freqs_here), loadings_block, noise_var)


def solution(mesh):
    placed = (P("sx", "sy", "af"), P("sx", "sy"), P("af", None), P("af", None), P("af", None))
    return jax.shard_map(
        body,
        mesh=mesh,
        in_specs=placed,
        out_specs=(P("sx", "sy", "af"), P("af", None), P()),
        check_vma=False,
    )
```

profile of v0, /device:TPU:32, one launch (start us, length us, event | category | flops | bytes accessed | tf_op | source)
XLA Modules:
  0.0 1608.8 jit_solution(8080160736587513446)
XLA Ops:
  19.1 3.8 collective-permute-start.2
  22.9 3.7 collective-permute-start.3
  26.8 12.6 all_gather.3
  47.2 3.8 custom-call.13
  51.0 29.7 %collective-permute-done.2 = f32[96,32,256]{2,1,0:T(8,128)} collective-permute-done((f32[96,32,256]{2,1,0:T(8,128)}, f32[96,32,256]{2,1,0:T(8,128)}, u32[]{:S(2)}, u32[]{:S(2)}) %collective-permute-start.2) | collective-permute-done | bytes 3145760 | tf_op jit(solution)/shard_map/ppermute | solution.py:16
  80.7 3.9 collective-permute-done.3
  84.7 5.9 pad_maximum_fusion
  90.6 11.6 copy.69
  104.7 38.0 %while.28 = (s32[]{:T(128)}, f32[32,96,256]{1,0,2:T(8,128)}, f32[256,65]{1,0:T(8,128)S(1)}, f32[96,96,256]{1,0,2:T(8,128)}, s32[96,32]{0,1:T(8,128)S(1)}, /*index=5*/s32[]{:T(128)}, s32[]{:T(128)}, s32[]{:T(128)}, s32[]{:T(128)}) while((s32[]{:T(128)}, f32[32,96,256]{1,0,2:T(8,128)}, f32[256,65]{1,0:T(8,128)S(1)}, ...), condition=%wide.region_1.0_spmd.clone, body=%wide.region_0.0_spmd.clone.sunk | while | flops 190322688 | bytes 2917519 | solution.py:62
  105.5 4.0 fusion.193
  110.2 4.0 fusion.193
  115.0 3.9 fusion.193
  119.7 3.9 fusion.193
  124.5 3.9 fusion.193
  129.2 3.9 fusion.193
  134.0 3.9 fusion.193
  138.7 3.9 fusion.193
  145.1 31.1 %while.29 = (s32[]{:T(128)}, f32[32,32,256]{0,1,2:T(8,128)}, f32[256,65]{1,0:T(8,128)S(1)}, f32[32,96,256]{1,0,2:T(8,128)}, s32[96,32]{0,1:T(8,128)S(1)}, /*index=5*/s32[]{:T(128)}, s32[]{:T(128)}, s32[]{:T(128)}, s32[]{:T(128)}) while((s32[]{:T(128)}, f32[32,32,256]{0,1,2:T(8,128)}, f32[256,65]{1,0:T(8,128)S(1)}, ...), condition=%wide.region_3.0_spmd.clone, body=%wide.region_2.0_spmd.clone.sunk | while | flops 114825224 | bytes 1868943 | solution.py:62
  176.2 4.7 copy.71
  180.9 4.3 all-to-all-start
  186.0 3.9 multiply_reduce_fusion
  189.9 6.2 all-to-all-done
  198.8 102.3 %all-reduce = (f32[32,32]{0,1:T(8,128)S(1)}, f32[]{:T(128)}) all-reduce(f32[32,32]{0,1:T(8,128)S(1)} %fusion.79, f32[]{:T(128)} %multiply_reduce_fusion), channel_id=1, replica_groups=mesh['sx'=8,'sy'=8,'af'=4] {'sx','sy','af'}, use_global_device_ids=true, to_apply=%region_7.10 | all-reduce | flops 1025 | bytes 8200 | tf_op jit(solution)/shard_map/psum | solution.py:88
  308.4 241.5 %all-reduce.6.cloned.1.call-done = f32[1024,32]{0,1:T(8,128)} async-done(((f32[1024,32]{0,1:T(8,128)}), f32[1024,32]{0,1:T(8,128)}) %all-reduce.6.cloned.1.call-update) | async-done | bytes 131088 | tf_op jit(solution)/shard_map/psum | solution.py:88
  564.8 75.9 %psum.67 = f32[32,32]{0,1:T(8,128)S(1)} all-reduce(f32[32,32]{0,1:T(8,128)S(1)} %fusion.85), channel_id=1, replica_groups=mesh['sx'=8,'sy'=8,'af'=4] {'sx','sy','af'}, use_global_device_ids=true, to_apply=%region_13.16 | all-reduce | flops 1024 | bytes 8192 | tf_op jit(solution)/shard_map/psum | solution.py:88
  648.0 240.3 %all-reduce.8.cloned.1.call-done = f32[1024,32]{0,1:T(8,128)} async-done(((f32[1024,32]{0,1:T(8,128)}), f32[1024,32]{0,1:T(8,128)}) %all-reduce.8.cloned.1.call-update) | async-done | bytes 131088 | tf_op jit(solution)/shard_map/psum | solution.py:88
  903.2 75.9 %psum.69 = f32[32,32]{0,1:T(8,128)S(1)} all-reduce(f32[32,32]{0,1:T(8,128)S(1)} %fusion.91), channel_id=1, replica_groups=mesh['sx'=8,'sy'=8,'af'=4] {'sx','sy','af'}, use_global_device_ids=true, to_apply=%region_17.20 | all-reduce | flops 1024 | bytes 8192 | tf_op jit(solution)/shard_map/psum | solution.py:88
  986.6 240.1 %all-reduce.10.cloned.1.call-done = f32[1024,32]{0,1:T(8,128)} async-done(((f32[1024,32]{0,1:T(8,128)}), f32[1024,32]{0,1:T(8,128)}) %all-reduce.10.cloned.1.call-update) | async-done | bytes 131088 | tf_op jit(solution)/shard_map/psum | solution.py:88
  1241.6 75.9 %psum.71 = f32[32,32]{0,1:T(8,128)S(1)} all-reduce(f32[32,32]{0,1:T(8,128)S(1)} %fusion.97), channel_id=1, replica_groups=mesh['sx'=8,'sy'=8,'af'=4] {'sx','sy','af'}, use_global_device_ids=true, to_apply=%region_21.24 | all-reduce | flops 1024 | bytes 8192 | tf_op jit(solution)/shard_map/psum | solution.py:88
  1324.8 240.3 %all-reduce.12.cloned.1.call-done = f32[1024,32]{0,1:T(8,128)} async-done(((f32[1024,32]{0,1:T(8,128)}), f32[1024,32]{0,1:T(8,128)}) %all-reduce.12.cloned.1.call-update) | async-done | bytes 131088 | tf_op jit(solution)/shard_map/psum | solution.py:88
  1580.5 4.0 all-to-all-start.1
  1585.1 15.1 all-to-all-done.1
  (174 shorter events, 148.8 us)
Async XLA Ops:
  7.9 18.7 %copy-start = (f32[256,65]{0,1:T(8,128)S(1)}, f32[256,65]{0,1:T(8,128)}, u32[]{:S(2)}) copy-start(f32[256,65]{0,1:T(8,128)} %param.14) | copy-start | bytes 199684
  7.9 18.8 %copy-start.1 = (f32[256,65]{0,1:T(8,128)S(1)}, f32[256,65]{0,1:T(8,128)}, u32[]{:S(2)}) copy-start(f32[256,65]{0,1:T(8,128)} %param.15) | copy-start | bytes 199684
  9.4 4.0 collective-permute-start
  11.2 5.9 collective-permute-start.1
  19.1 61.7 %collective-permute-start.2 = (f32[96,32,256]{2,1,0:T(8,128)}, f32[96,32,256]{2,1,0:T(8,128)}, u32[]{:S(2)}, u32[]{:S(2)}) collective-permute-start(f32[96,32,256]{2,1,0:T(8,128)} %pad_maximum_fusion.1), channel_id=1, source_target_pairs={{0,4},{4,8},{8,12},{12,16},{16,20},{20,24},{24,28},{1,5},{5,9},{9,... | collective-permute-start | bytes 9437192 | tf_op jit(solution)/shard_map/ppermute | solution.py:16
  22.9 61.8 %collective-permute-start.3 = (f32[96,32,256]{2,1,0:T(8,128)}, f32[96,32,256]{2,1,0:T(8,128)}, u32[]{:S(2)}, u32[]{:S(2)}) collective-permute-start(f32[96,32,256]{2,1,0:T(8,128)} %pad_maximum_fusion.1), channel_id=1, source_target_pairs={{4,0},{8,4},{12,8},{16,12},{20,16},{24,20},{28,24},{5,1},{9,5},{13... | collective-permute-start | bytes 9437192 | tf_op jit(solution)/shard_map/ppermute | solution.py:19
  176.2 9.0 copy-start.2
  180.9 15.2 all-to-all-start
  185.2 364.7 %all-reduce.6.cloned.1.call-start = ((), (), s32[]{:S(2)}) async-start(), calls=%async_computation.2 | async-start | bytes 262144 | tf_op jit(solution)/shard_map/psum | solution.py:88
  308.1 580.1 %all-reduce.8.cloned.1.call-start = ((), (), s32[]{:S(2)}) async-start(), calls=%async_computation.3 | async-start | bytes 262144 | tf_op jit(solution)/shard_map/psum | solution.py:88
  647.7 579.0 %all-reduce.10.cloned.1.call-start = ((), (), s32[]{:S(2)}) async-start(), calls=%async_computation.4 | async-start | bytes 262144 | tf_op jit(solution)/shard_map/psum | solution.py:88
  986.1 579.0 %all-reduce.12.cloned.1.call-start = ((), (), s32[]{:S(2)}) async-start(), calls=%async_computation.5 | async-start | bytes 262144 | tf_op jit(solution)/shard_map/psum | solution.py:88
  1580.5 19.7 %all-to-all-start.1 = ((f32[256,4,256]{2,0,1:T(8,128)}), f32[256,4,256]{2,0,1:T(8,128)S(1)}, u32[]{:S(2)}, u32[]{:S(2)}) async-start(f32[256,4,256]{2,0,1:T(8,128)} %bitcast.179), calls=%async_computation.1 | async-start | bytes 2097152 | tf_op jit(solution)/shard_map/all_to_all | solution.py:105
Sparse Core Ops, SparseCore 0:
  308.2 241.6 all-reduce.5
  647.8 240.3 all-reduce.7
  986.2 240.4 all-reduce.9
  1324.7 240.3 all-reduce.11
where the time goes:
time: 1610 us
  waiting for transfers between devices  1020 us (63%)
  blocking collectives  342 us (21%)
  matrix products  98 us (6%)
  other arithmetic  78.2 us (5%)
  local copies, waits for them, and re-layouts  25.8 us (2%)
  between operations  23.1 us (1%)
  starting transfers between devices  19.2 us (1%)
    psum x4, waiting for transfers between devices, body(): lax.psum((contract_rows(pixel_rows, latent), contract_rows(latent, latent...  962 us
    psum x4, blocking collectives, body(): lax.psum((contract_rows(pixel_rows, latent), contract_rows(latent, latent...  330 us
    another operation x27, other arithmetic, inverse_spd(): factor = jnp.linalg.cholesky(matrix)  33.1 us
  transfers between devices with their start and end apart: 10, of which 10 were waited for; matrix products, arithmetic and copies ran while one was open for 1% of the time, Pallas kernels for 0%

commit v1 on v0

--- a/solution.py
+++ b/solution.py
@@ -85,8 +85,13 @@
             jnp.dot(loadings, inverse, precision=HIGHEST_PRECISION),
             precision=HIGHEST_PRECISION,
         )
-        cross_moment, second = lax.psum(
-            (contract_rows(pixel_rows, latent), contract_rows(latent, latent)), ("sx", "sy", "af")
+
+        def _enter_quarters(mine, lane_axis, ax_name):
+            o_now = lax.psum(lax.psum(mine, lane_axis), axis_name=ax_name)
+            return o_now
+
+        cross_moment, second = _enter_quarters(
+            (contract_rows(pixel_rows, latent), contract_rows(latent, latent)), "sx", ("sy", "af")
         )
         scaled = pixel_count * noise_var * inverse + second
         updated = jnp.dot(cross_moment, inverse_spd(scaled), precision=HIGHEST_PRECISION)

time: 1610 us -> 1880 us (1.17)
  blocking collectives: 342 us -> 748 us
  waiting for transfers between devices: 1020 us -> 888 us
    psum x4 -> x9, blocking collectives: 330 us -> 735 us  [the longest x8 634 us: _enter_quarters(): o_now = lax.psum(lax.psum(mine, lane_axis), axis_name=ax_name)]
    psum x4 -> x8, waiting for transfers between devices: 962 us -> 839 us  [_enter_quarters(): o_now = lax.psum(lax.psum(mine, lane_axis), axis_name=ax_name)]
  transfers between devices with their start and end apart: 10 -> 14, of which waited for: 10 -> 13; matrix products, arithmetic and copies ran while one was open for 1% -> 1% of each run, Pallas kernels for 0% -> 0%
where the time goes in v1:
time: 1880 us
  waiting for transfers between devices  888 us (47%)
  blocking collectives  748 us (40%)
  matrix products  97.8 us (5%)
  other arithmetic  78.2 us (4%)
  local copies, waits for them, and re-layouts  25.8 us (1%)
  between operations  23.4 us (1%)
  starting transfers between devices  19.6 us (1%)
    psum x8, waiting for transfers between devices, _enter_quarters(): o_now = lax.psum(lax.psum(mine, lane_axis), axis_name=ax_name)  839 us
    psum x8, blocking collectives, _enter_quarters(): o_now = lax.psum(lax.psum(mine, lane_axis), axis_name=ax_name)  634 us
    psum x1, blocking collectives, body(): total_power = lax.psum(jnp.sum(spectra * spectra), ('sx', 'sy', 'af'))  101 us
  transfers between devices with their start and end apart: 14, of which 13 were waited for; matrix products, arithmetic and copies ran while one was open for 1% of the time, Pallas kernels for 0%

profile of v1, /device:TPU:32, one launch (start us, length us, event | category | flops | bytes accessed | tf_op | source)
XLA Modules:
  0.0 1880.7 jit_solution(13578796029791170810)
XLA Ops:
  26.8 12.6 all_gather.3
  51.0 29.7 %collective-permute-done.2 = f32[96,32,256]{2,1,0:T(8,128)} collective-permute-done((f32[96,32,256]{2,1,0:T(8,128)}, f32[96,32,256]{2,1,0:T(8,128)}, u32[]{:S(2)}, u32[]{:S(2)}) %collective-permute-start.2) | collective-permute-done | bytes 3145760 | tf_op jit(solution)/shard_map/ppermute | solution.py:16
  84.7 5.9 pad_maximum_fusion
  90.6 11.6 copy.69
  104.7 38.0 %while.28 = (s32[]{:T(128)}, f32[32,96,256]{1,0,2:T(8,128)}, f32[256,65]{1,0:T(8,128)S(1)}, f32[96,96,256]{1,0,2:T(8,128)}, s32[96,32]{0,1:T(8,128)S(1)}, /*index=5*/s32[]{:T(128)}, s32[]{:T(128)}, s32[]{:T(128)}, s32[]{:T(128)}) while((s32[]{:T(128)}, f32[32,96,256]{1,0,2:T(8,128)}, f32[256,65]{1,0:T(8,128)S(1)}, ...), condition=%wide.region_1.0_spmd.clone, body=%wide.region_0.0_spmd.clone.sunk | while | flops 190322688 | bytes 2917519 | solution.py:62
  105.5 4.0 fusion.193
  110.2 4.0 fusion.193
  124.5 3.9 fusion.193
  129.2 3.9 fusion.193
  138.7 3.9 fusion.193
  145.1 31.1 %while.29 = (s32[]{:T(128)}, f32[32,32,256]{0,1,2:T(8,128)}, f32[256,65]{1,0:T(8,128)S(1)}, f32[32,96,256]{1,0,2:T(8,128)}, s32[96,32]{0,1:T(8,128)S(1)}, /*index=5*/s32[]{:T(128)}, s32[]{:T(128)}, s32[]{:T(128)}, s32[]{:T(128)}) while((s32[]{:T(128)}, f32[32,32,256]{0,1,2:T(8,128)}, f32[256,65]{1,0:T(8,128)S(1)}, ...), condition=%wide.region_3.0_spmd.clone, body=%wide.region_2.0_spmd.clone.sunk | while | flops 114825224 | bytes 1868943 | solution.py:62
  176.2 4.7 copy.71
  180.9 4.3 all-to-all-start
  189.9 100.9 %psum.123 = f32[]{:T(128)} all-reduce(f32[]{:T(128)} %multiply_reduce_fusion), channel_id=1, replica_groups=mesh['sx'=8,'sy'=8,'af'=4] {'sx','sy','af'}, use_global_device_ids=true, to_apply=%region_11.14 | all-reduce | flops 1 | bytes 8 | tf_op jit(solution)/shard_map/psum | solution.py:73
  293.5 23.6 %psum.121 = f32[32,32]{0,1:T(8,128)S(1)} all-reduce(f32[32,32]{0,1:T(8,128)S(1)} %fusion.79), channel_id=1, replica_groups=mesh['sx'=8,'sy'=8,'af'=4] {'sx'}, use_global_device_ids=true, to_apply=%region_8.11 | all-reduce | flops 1024 | bytes 8192 | tf_op jit(solution)/shard_map/psum | solution.py:90
  317.1 134.7 %psum.122 = f32[32,32]{0,1:T(8,128)S(1)} all-reduce(f32[32,32]{0,1:T(8,128)S(1)} %psum.121), channel_id=1, replica_groups=mesh['sx'=8,'sy'=8,'af'=4] {'sy','af'}, use_global_device_ids=true, to_apply=%region_9.12 | all-reduce | flops 1024 | bytes 8192 | tf_op jit(solution)/shard_map/psum | solution.py:90
  458.9 65.5 %all-reduce.9.cloned.1.call-done = f32[1024,32]{0,1:T(8,128)} async-done(((f32[1024,32]{0,1:T(8,128)}), f32[1024,32]{0,1:T(8,128)}) %all-reduce.9.cloned.1.call-update) | async-done | bytes 131088 | tf_op jit(solution)/shard_map/psum | solution.py:90
  524.7 144.4 %all-reduce.11.cloned.1.call-done = f32[1024,32]{0,1:T(8,128)} async-done(((f32[1024,32]{0,1:T(8,128)}), f32[1024,32]{0,1:T(8,128)}) %all-reduce.11.cloned.1.call-update) | async-done | bytes 131088 | tf_op jit(solution)/shard_map/psum | solution.py:90
  684.0 23.5 %psum.126 = f32[32,32]{0,1:T(8,128)S(1)} all-reduce(f32[32,32]{0,1:T(8,128)S(1)} %fusion.85), channel_id=1, replica_groups=mesh['sx'=8,'sy'=8,'af'=4] {'sx'}, use_global_device_ids=true, to_apply=%region_16.19 | all-reduce | flops 1024 | bytes 8192 | tf_op jit(solution)/shard_map/psum | solution.py:90
  707.6 135.1 %psum.127 = f32[32,32]{0,1:T(8,128)S(1)} all-reduce(f32[32,32]{0,1:T(8,128)S(1)} %psum.126), channel_id=1, replica_groups=mesh['sx'=8,'sy'=8,'af'=4] {'sy','af'}, use_global_device_ids=true, to_apply=%region_17.20 | all-reduce | flops 1024 | bytes 8192 | tf_op jit(solution)/shard_map/psum | solution.py:90
  849.7 65.5 %all-reduce.13.cloned.1.call-done = f32[1024,32]{0,1:T(8,128)} async-done(((f32[1024,32]{0,1:T(8,128)}), f32[1024,32]{0,1:T(8,128)}) %all-reduce.13.cloned.1.call-update) | async-done | bytes 131088 | tf_op jit(solution)/shard_map/psum | solution.py:90
  915.5 144.3 %all-reduce.15.cloned.1.call-done = f32[1024,32]{0,1:T(8,128)} async-done(((f32[1024,32]{0,1:T(8,128)}), f32[1024,32]{0,1:T(8,128)}) %all-reduce.15.cloned.1.call-update) | async-done | bytes 131088 | tf_op jit(solution)/shard_map/psum | solution.py:90
  1074.7 23.5 %psum.130 = f32[32,32]{0,1:T(8,128)S(1)} all-reduce(f32[32,32]{0,1:T(8,128)S(1)} %fusion.91), channel_id=1, replica_groups=mesh['sx'=8,'sy'=8,'af'=4] {'sx'}, use_global_device_ids=true, to_apply=%region_22.25 | all-reduce | flops 1024 | bytes 8192 | tf_op jit(solution)/shard_map/psum | solution.py:90
  1098.3 135.1 %psum.131 = f32[32,32]{0,1:T(8,128)S(1)} all-reduce(f32[32,32]{0,1:T(8,128)S(1)} %psum.130), channel_id=1, replica_groups=mesh['sx'=8,'sy'=8,'af'=4] {'sy','af'}, use_global_device_ids=true, to_apply=%region_23.26 | all-reduce | flops 1024 | bytes 8192 | tf_op jit(solution)/shard_map/psum | solution.py:90
  1240.4 65.5 %all-reduce.17.cloned.1.call-done = f32[1024,32]{0,1:T(8,128)} async-done(((f32[1024,32]{0,1:T(8,128)}), f32[1024,32]{0,1:T(8,128)}) %all-reduce.17.cloned.1.call-update) | async-done | bytes 131088 | tf_op jit(solution)/shard_map/psum | solution.py:90
  1306.4 144.1 %all-reduce.19.cloned.1.call-done = f32[1024,32]{0,1:T(8,128)} async-done(((f32[1024,32]{0,1:T(8,128)}), f32[1024,32]{0,1:T(8,128)}) %all-reduce.19.cloned.1.call-update) | async-done | bytes 131088 | tf_op jit(solution)/shard_map/psum | solution.py:90
  1465.4 23.5 %psum.134 = f32[32,32]{0,1:T(8,128)S(1)} all-reduce(f32[32,32]{0,1:T(8,128)S(1)} %fusion.97), channel_id=1, replica_groups=mesh['sx'=8,'sy'=8,'af'=4] {'sx'}, use_global_device_ids=true, to_apply=%region_28.31 | all-reduce | flops 1024 | bytes 8192 | tf_op jit(solution)/shard_map/psum | solution.py:90
  1488.9 135.1 %psum.135 = f32[32,32]{0,1:T(8,128)S(1)} all-reduce(f32[32,32]{0,1:T(8,128)S(1)} %psum.134), channel_id=1, replica_groups=mesh['sx'=8,'sy'=8,'af'=4] {'sy','af'}, use_global_device_ids=true, to_apply=%region_29.32 | all-reduce | flops 1024 | bytes 8192 | tf_op jit(solution)/shard_map/psum | solution.py:90
  1631.1 65.5 %all-reduce.21.cloned.1.call-done = f32[1024,32]{0,1:T(8,128)} async-done(((f32[1024,32]{0,1:T(8,128)}), f32[1024,32]{0,1:T(8,128)}) %all-reduce.21.cloned.1.call-update) | async-done | bytes 131088 | tf_op jit(solution)/shard_map/psum | solution.py:90
  1696.8 144.5 %all-reduce.23.cloned.1.call-done = f32[1024,32]{0,1:T(8,128)} async-done(((f32[1024,32]{0,1:T(8,128)}), f32[1024,32]{0,1:T(8,128)}) %all-reduce.23.cloned.1.call-update) | async-done | bytes 131088 | tf_op jit(solution)/shard_map/psum | solution.py:90
  1856.7 4.2 all-to-all-start.1
  1861.5 10.3 all-to-all-done.1
  (191 shorter events, 179.8 us)
Async XLA Ops:
  7.9 18.7 copy-start
  7.9 18.8 %copy-start.1 = (f32[256,65]{0,1:T(8,128)S(1)}, f32[256,65]{0,1:T(8,128)}, u32[]{:S(2)}) copy-start(f32[256,65]{0,1:T(8,128)} %param.15) | copy-start | bytes 199684
  9.4 4.0 collective-permute-start
  11.2 5.9 collective-permute-start.1
  19.1 61.7 %collective-permute-start.2 = (f32[96,32,256]{2,1,0:T(8,128)}, f32[96,32,256]{2,1,0:T(8,128)}, u32[]{:S(2)}, u32[]{:S(2)}) collective-permute-start(f32[96,32,256]{2,1,0:T(8,128)} %pad_maximum_fusion.1), channel_id=1, source_target_pairs={{0,4},{4,8},{8,12},{12,16},{16,20},{20,24},{24,28},{1,5},{5,9},{9,... | collective-permute-start | bytes 9437192 | tf_op jit(solution)/shard_map/ppermute | solution.py:16
  22.9 61.8 %collective-permute-start.3 = (f32[96,32,256]{2,1,0:T(8,128)}, f32[96,32,256]{2,1,0:T(8,128)}, u32[]{:S(2)}, u32[]{:S(2)}) collective-permute-start(f32[96,32,256]{2,1,0:T(8,128)} %pad_maximum_fusion.1), channel_id=1, source_target_pairs={{4,0},{8,4},{12,8},{16,12},{20,16},{24,20},{28,24},{5,1},{9,5},{13... | collective-permute-start | bytes 9437192 | tf_op jit(solution)/shard_map/ppermute | solution.py:19
  176.2 9.0 copy-start.2
  180.9 109.9 %all-to-all-start = ((f32[4,256,256]{2,1,0:T(8,128)}), f32[4,256,256]{2,1,0:T(8,128)S(1)}, u32[]{:S(2)}, u32[]{:S(2)}) async-start(f32[4,256,256]{2,1,0:T(8,128)} %bitcast), calls=%async_computation | async-start | bytes 2097152 | tf_op jit(solution)/shard_map/all_to_all | solution.py:80
  185.2 339.2 %all-reduce.9.cloned.1.call-start = ((), (), s32[]{:S(2)}) async-start(), calls=%async_computation.2 | async-start | bytes 262144 | tf_op jit(solution)/shard_map/psum | solution.py:90
  458.6 210.5 %all-reduce.11.cloned.1.call-start = ((), (), s32[]{:S(2)}) async-start(), calls=%async_computation.3 | async-start | bytes 262144 | tf_op jit(solution)/shard_map/psum | solution.py:90
  524.4 390.8 %all-reduce.13.cloned.1.call-start = ((), (), s32[]{:S(2)}) async-start(), calls=%async_computation.4 | async-start | bytes 262144 | tf_op jit(solution)/shard_map/psum | solution.py:90
  849.5 210.3 %all-reduce.15.cloned.1.call-start = ((), (), s32[]{:S(2)}) async-start(), calls=%async_computation.5 | async-start | bytes 262144 | tf_op jit(solution)/shard_map/psum | solution.py:90
  915.3 390.7 %all-reduce.17.cloned.1.call-start = ((), (), s32[]{:S(2)}) async-start(), calls=%async_computation.6 | async-start | bytes 262144 | tf_op jit(solution)/shard_map/psum | solution.py:90
  1240.2 210.3 %all-reduce.19.cloned.1.call-start = ((), (), s32[]{:S(2)}) async-start(), calls=%async_computation.7 | async-start | bytes 262144 | tf_op jit(solution)/shard_map/psum | solution.py:90
  1305.9 390.7 %all-reduce.21.cloned.1.call-start = ((), (), s32[]{:S(2)}) async-start(), calls=%async_computation.8 | async-start | bytes 262144 | tf_op jit(solution)/shard_map/psum | solution.py:90
  1630.8 210.5 %all-reduce.23.cloned.1.call-start = ((), (), s32[]{:S(2)}) async-start(), calls=%async_computation.9 | async-start | bytes 262144 | tf_op jit(solution)/shard_map/psum | solution.py:90
  1856.7 15.1 all-to-all-start.1
Sparse Core Ops, SparseCore 0:
  458.8 65.5 all-reduce.8
  527.9 141.2 all-reduce.10
  849.6 65.5 all-reduce.12
  918.5 141.2 all-reduce.14
  1240.3 65.5 all-reduce.16
  1309.2 141.2 all-reduce.18
  1631.0 65.5 all-reduce.20
  1700.0 141.2 all-reduce.22
